TPU v7x, 16 devices: a 4x2x1 block of a 4x4x8 slice. The times are simulated.
16 devices in a mesh: dp: 4 (over y, z, core), tp: 4 (over x).
Axes of the slice: x: 4, y: 2, z: 1, core: 2. Of those that a mesh axis runs over, the one named last changes fastest.
The devices are a block of a 4x4x8 slice.
Arguments:
- x: bfloat16 [8192, 3072], P('dp'), parts along dimension 0
- dy: bfloat16 [8192, 3072], P('dp'), parts along dimension 0
- gate: bfloat16 [8192, 8192], P('dp', 'tp'), parts along dimension 0
- up: bfloat16 [8192, 8192], P('dp', 'tp'), parts along dimension 0
- w_gate: bfloat16 [3072, 8192], P(None, 'tp')
- w_up: bfloat16 [3072, 8192], P(None, 'tp')
- w_down: bfloat16 [8192, 3072], P('tp')
Outputs:
- output 1: bfloat16 [8192, 3072], P('dp'), parts along dimension 0
- output 2: bfloat16 [12288, 8192], P('dp', 'tp'), parts along dimension 0
- output 3: bfloat16 [12288, 8192], P('dp', 'tp'), parts along dimension 0
- output 4: bfloat16 [32768, 3072], P(('dp', 'tp')), parts along dimension 0
There are 4 independent parts. A program takes and returns all parts, laid end to end along the dimension named above; an argument that names none is the same for every part.
All inputs are finite; a program needn't handle non-finite values.
Results may differ from a plain program's by a relative error of at most 0.012.
Values are sent between devices in bfloat16 or wider.
A program may use at most 768 MiB of HBM per device.

v0:
```python
import jax
import jax.numpy as jnp
from jax import lax
from jax.sharding import PartitionSpec as P


def act(gate, up):
    return jax.nn.silu(gate) * up


def solution(mesh):
    def step(x, dy, gate, up, w_gate, w_up, w_down):
        hidden, back = jax.vjp(act, gate.astype(jnp.float32), up.astype(jnp.float32))
        d_hidden = jnp.dot(dy, w_down.T, preferred_element_type=jnp.float32)
        d_gate, d_up = (g.astype(jnp.bfloat16) for g in back(d_hidden))
        term = jnp.dot(d_gate, w_gate.T, preferred_element_type=jnp.float32) + jnp.dot(d_up, w_up.T, preferred_element_type=jnp.float32)
        dx = lax.psum(term.astype(jnp.bfloat16), "tp")
        dw_gate = jnp.dot(x.T, d_gate, preferred_element_type=jnp.float32)
        dw_up = jnp.dot(x.T, d_up, preferred_element_type=jnp.float32)
        dw_down = jnp.dot(hidden.astype(jnp.bfloat16).T, dy, preferred_element_type=jnp.float32)
        return dx, *(g.astype(jnp.bfloat16) for g in (dw_gate, dw_up, dw_down))

    tokens, columns, rows = P("dp", None), P(None, "tp"), P("tp", None)
    return jax.shard_map(
        step,
        mesh=mesh,
        in_specs=(tokens, tokens, P("dp", "tp"), P("dp", "tp"), columns, columns, rows),
        out_specs=(tokens, P("dp", "tp"), P("dp", "tp"), P(("dp", "tp"), None)),
        check_vma=False,
    )
```

profile of v0, /device:TPU:112, one launch (start us, length us, event | category | flops | bytes accessed | tf_op | source)
XLA Modules:
  0.0 362.0 jit_solution(18440489266094166044)
XLA Ops:
  7.2 0.1 all-reduce.2.cloned.1.call-start
  7.2 43.2 %fusion.6 = (bf16[2048,2048]{1,0:T(8,128)(2,1)}, f32[2048,2048]{1,0:T(8,128)}) fusion(bf16[2048,2048]{1,0:T(8,128)(2,1)} %param.9, bf16[2048,2048]{1,0:T(8,128)(2,1)} %param.10, bf16[2048,3072]{1,0:T(8,128)(2,1)} %param.8, bf16[2048,3072]{1,0:T(8,128)(2,1)} %param.13), kind=kOutput, calls=%fused_computation.13 | convolution fusion | flops 25824329728 | bytes 67108864 | tf_op jit(solution)/shard_map/dot_general | solution.py:14
  50.4 34.4 %fusion.9 = f32[2048,3072]{1,0:T(8,128)} fusion(bf16[2048,2048]{1,0:T(8,128)(2,1)} %get-tuple-element.8, bf16[3072,2048]{1,0:T(8,128)(2,1)} %param.11), kind=kOutput, calls=%fused_computation.19 | convolution fusion | flops 25769803776 | bytes 46137344 | tf_op jit(solution)/shard_map/dot_general | solution.py:16
  84.8 36.9 %add_convert_fusion = bf16[2048,3072]{1,0:T(8,128)(2,1)} fusion(f32[2048,3072]{1,0:T(8,128)} %fusion.9, bf16[3072,2048]{1,0:T(8,128)(2,1)} %param.12, f32[2048,2048]{1,0:T(8,128)} %get-tuple-element.9, bf16[2048,2048]{1,0:T(8,128)(2,1)} %param.9), kind=kOutput, calls=%fused_computation | convolution fusion | flops 25811746816 | bytes 75497472 | tf_op jit(solution)/shard_map/dot_general | solution.py:16
  121.8 0.1 all-reduce.2.cloned.1.call-update
  121.8 0.0 copy-start
  121.8 39.1 %convert_bitcast_fusion = bf16[3072,2048]{0,1:T(8,128)(2,1)} fusion(bf16[2048,3072]{1,0:T(8,128)(2,1)} %param.7, f32[2048,2048]{1,0:T(8,128)} %get-tuple-element.9, bf16[2048,2048]{1,0:T(8,128)(2,1)} %param.9), kind=kOutput, calls=%fused_computation.15 | convolution fusion | flops 25805455360 | bytes 50331648 | tf_op jit(solution)/shard_map/dot_general | solution.py:19
  160.9 0.0 copy-done
  160.9 30.7 %convert_bitcast_fusion.1 = bf16[3072,2048]{0,1:T(8,128)(2,1)} fusion(bf16[2048,2048]{1,0:T(8,128)(2,1)} %get-tuple-element.8, bf16[2048,3072]{1,0:T(8,128)(2,1)S(1)} %copy-done), kind=kOutput, calls=%fused_computation.16 | convolution fusion | flops 25776095232 | bytes 33554432 | tf_op jit(solution)/shard_map/dot_general | solution.py:18
  191.6 16.6 %copy.11 = bf16[3072,2048]{1,0:T(8,128)(2,1)} copy(bf16[3072,2048]{0,1:T(8,128)(2,1)} %convert_bitcast_fusion.1) | data formatting | bytes 25165824
  208.2 16.6 %copy.12 = bf16[3072,2048]{1,0:T(8,128)(2,1)} copy(bf16[3072,2048]{0,1:T(8,128)(2,1)} %convert_bitcast_fusion) | data formatting | bytes 25165824
  224.8 36.8 %convolution_convert_fusion = bf16[2048,3072]{1,0:T(8,128)(2,1)} fusion(bf16[2048,3072]{1,0:T(8,128)(2,1)} %param.8, bf16[2048,2048]{1,0:T(8,128)(2,1)} %param.10, bf16[2048,2048]{1,0:T(8,128)(2,1)} %param.9), kind=kOutput, calls=%fused_computation.17 | convolution fusion | flops 25809649664 | bytes 41943040 | tf_op jit(solution)/shard_map/dot_general | solution.py:20
  261.5 82.9 %all-reduce.2.cloned.1.call-done = bf16[2048,3072]{1,0:T(8,128)(2,1)} async-done(((bf16[2048,3072]{1,0:T(8,128)(2,1)}), bf16[2048,3072]{1,0:T(8,128)(2,1)}) %all-reduce.2.cloned.1.call-update) | async-done | bytes 12582928 | tf_op jit(solution)/shard_map/psum | solution.py:17
  344.4 10.5 %copy.14 = bf16[2048,3072]{1,0:T(8,128)(2,1)} copy(bf16[2048,3072]{1,0:T(8,128)(2,1)} %all-reduce.2.cloned.1.call-done) | data formatting | bytes 25165824
Async XLA Ops:
  7.2 337.2 %all-reduce.2.cloned.1.call-start = ((), (), s32[]{:S(2)}) async-start(), calls=%async_computation | async-start | bytes 25165824 | tf_op jit(solution)/shard_map/psum | solution.py:17
  121.8 39.1 %copy-start = (bf16[2048,3072]{1,0:T(8,128)(2,1)S(1)}, bf16[2048,3072]{1,0:T(8,128)(2,1)}, u32[]{:S(2)}) copy-start(bf16[2048,3072]{1,0:T(8,128)(2,1)} %param.7) | copy-start | bytes 37748740
Sparse Core Ops, SparseCore 0:
  121.9 222.4 all-reduce.1
where the time goes:
time: 369 us; the launch traced here: 362 us
  matrix products  221 us (60%)
  waiting for transfers between devices  82.9 us (22%)
  local copies, waits for them, and re-layouts  43.7 us (12%)
  between operations  14.3 us (4%)
    psum x1, waiting for transfers between devices, step(): dx = lax.psum(term.astype(jnp.bfloat16), 'tp')  82.9 us
    unnamed x5, local copies, waits for them, and re-layouts  43.7 us
    dot_general x1, matrix products, step(): d_hidden = jnp.dot(dy, w_down.T, preferred_element_type=jnp.float32)  43.2 us
    dot_general x1, matrix products, step(): dw_up = jnp.dot(x.T, d_up, preferred_element_type=jnp.float32)  39.1 us
    dot_general x1, matrix products, step(): jnp.dot(d_up, w_up.T, preferred_element_type=jnp.float32)  36.9 us
    dot_general x1, matrix products, step(): jnp.dot(hidden.astype(jnp.bfloat16).T, dy, preferred_element_type=jnp.flo...  36.8 us
    dot_general x1, matrix products, step(): jnp.dot(d_gate, w_gate.T, preferred_element_type=jnp.float32)  34.4 us
    dot_general x1, matrix products, step(): dw_gate = jnp.dot(x.T, d_gate, preferred_element_type=jnp.float32)  30.7 us
  transfers between devices with their start and end apart: 1, of which 1 were waited for; matrix products, arithmetic and copies ran while one was open for 39% of the time, Pallas kernels for 0%

commit v1 on v0

v1 whole, which is shorter than its diff:
```python
import functools

import jax
import jax.numpy as jnp
from jax import lax
from jax.experimental import pallas as pl
from jax.experimental.pallas import tpu as pltpu
from jax.sharding import PartitionSpec as P


BF16, F32 = jnp.bfloat16, jnp.float32
MESH = pl.DeviceIdType.MESH
VMEM_LIMIT = 66_000_000
UNIT = 128
FT = 512
DT = 512
MT, CT = 512, 512


def dot_nt(a, b):
    return lax.dot_general(a, b, (((1,), (1,)), ((), ())), preferred_element_type=F32)


def dot_tn(a, b):
    return lax.dot_general(a, b, (((0,), (0,)), ((), ())), preferred_element_type=F32)


def backward_reduce_scatter(
    n, axis,
    dy_ref, gate_ref, up_ref, wg_ref, wu_ref, wd_ref,
    dg_ref, du_ref, hid_ref, top_ref, bot_ref,
    dy_v, gate_v, up_v, dg_v, du_v, hid_v, wg_v, wu_v, wd_v, ring,
    in_sem, out_sem, w_sem, own_sem, send_sem, recv_sem,
):
    rows, width = dy_ref.shape
    hidden = gate_ref.shape[1]
    block = rows // n
    half = block // 2
    units = half // UNIT
    steps_f, pieces = hidden // FT, width // DT
    chunks = n * units

    me = lax.axis_index(axis)
    right, left = lax.rem(me + 1, n), lax.rem(me + n - 1, n)

    def first_rows(c):
        s, u = c // units, lax.rem(c, units)
        cw = lax.rem(me + 2 * n - 1 - s, n) * block + u * UNIT
        ccw = lax.rem(me + 1 + s, n) * block + half + u * UNIT
        return pl.multiple_of(cw, UNIT), pl.multiple_of(ccw, UNIT)

    def loads(c):
        slot = lax.rem(c, 2)
        out = []
        for d, start in enumerate(first_rows(c)):
            for k, (src, dst) in enumerate(((dy_ref, dy_v), (gate_ref, gate_v), (up_ref, up_v))):
                out.append(pltpu.make_async_copy(
                    src.at[pl.ds(start, UNIT)], dst.at[slot, pl.ds(d * UNIT, UNIT)], in_sem.at[slot, d, k]))
        return out

    def stores(c):
        out = []
        for d, start in enumerate(first_rows(c)):
            for k, (src, dst) in enumerate(((dg_v, dg_ref), (du_v, du_ref), (hid_v, hid_ref))):
                out.append(pltpu.make_async_copy(
                    src.at[pl.ds(d * UNIT, UNIT)], dst.at[pl.ds(start, UNIT)], out_sem.at[d, k]))
        return out

    def weights(g):
        if g < steps_f:
            part = pl.ds(g * FT, FT)
            return [pltpu.make_async_copy(wd_ref.at[part], wd_v.at[part], w_sem.at[g, 0])]
        part = pl.ds((g - steps_f) * DT, DT)
        return [pltpu.make_async_copy(src.at[part], dst.at[part], w_sem.at[g, k])
                for k, (src, dst) in enumerate(((wg_ref, wg_v), (wu_ref, wu_v)))]

    groups = steps_f + pieces

    def remote(d, s, u, h):
        return pltpu.make_async_remote_copy(
            src_ref=ring.at[d, s, u, h], dst_ref=ring.at[d, s + 1, u, h],
            send_sem=send_sem.at[d, s, u, h], recv_sem=recv_sem.at[d, s, u, h],
            device_id={axis: right if d == 0 else left}, device_id_type=MESH)

    def own(d, u, h):
        dst = (top_ref, bot_ref)[d]
        return pltpu.make_async_copy(
            ring.at[d, n - 1, u, h],
            dst.at[pl.ds(u * UNIT, UNIT), pl.ds(h * DT, DT)], own_sem.at[d, u, h])

    for copy in loads(0):
        copy.start()
    ahead = 3
    for g in range(ahead):
        for copy in weights(g):
            copy.start()

    barrier = pltpu.get_barrier_semaphore()
    for other in (left, right):
        pl.semaphore_signal(barrier, inc=1, device_id={axis: other}, device_id_type=MESH)
    ring[:, 0] = jnp.zeros_like(ring[:, 0])
    pl.semaphore_wait(barrier, 2)

    @pl.loop(0, chunks)
    def _(c):
        s, u = c // units, lax.rem(c, units)
        slot = lax.rem(c, 2)

        @pl.when(c + 1 < chunks)
        def _():
            for copy in loads(c + 1):
                copy.start()

        for copy in loads(c):
            copy.wait()

        @pl.when(c > 0)
        def _():
            for copy in stores(c - 1):
                copy.wait()

        def weights_here(g):
            @pl.when(c == 0)
            def _():
                for copy in weights(g):
                    copy.wait()
                if g + ahead < groups:
                    for copy in weights(g + ahead):
                        copy.start()

        for f in range(steps_f):
            weights_here(f)
            cols = pl.ds(f * FT, FT)
            dh = dot_nt(dy_v[slot], wd_v[cols, :])
            gate = gate_v[slot, :, cols].astype(F32)
            up = up_v[slot, :, cols].astype(F32)
            sig = jax.nn.sigmoid(gate)
            act = gate * sig
            hid_v[:, cols] = (act * up).astype(BF16)
            du_v[:, cols] = (dh * act).astype(BF16)
            dg_v[:, cols] = (dh * up * (sig + act * (1.0 - sig))).astype(BF16)

        for copy in stores(c):
            copy.start()

        for h in range(pieces):
            weights_here(steps_f + h)

            @pl.when(s > 0)
            def _():
                for d in range(2):
                    remote(d, s - 1, u, h).wait_recv()

            cols = pl.ds(h * DT, DT)
            term = dot_nt(dg_v[...], wg_v[cols, :]) + dot_nt(du_v[...], wu_v[cols, :])
            for d in range(2):
                ring[d, s, u, h] = (ring[d, s, u, h].astype(F32) + term[d * UNIT:(d + 1) * UNIT]).astype(BF16)

            @pl.when(s < n - 1)
            def _():
                for d in range(2):
                    remote(d, s, u, h).start()

            @pl.when(s == n - 1)
            def _():
                for d in range(2):
                    own(d, u, h).start()

    for copy in stores(chunks - 1):
        copy.wait()

    @pl.loop(0, units)
    def _(u):
        for d in range(2):
            for h in range(pieces):
                own(d, u, h).wait()

    @pl.loop(0, (n - 1) * units)
    def _(c):
        for d in range(2):
            for h in range(pieces):
                remote(d, c // units, lax.rem(c, units), h).wait_send()


def reduce_scatter_call(n, axis, dy, gate, up, wg, wu, wd):
    rows, width = dy.shape
    hidden = gate.shape[1]
    half = rows // n // 2
    units, pieces, groups = half // UNIT, width // DT, hidden // FT + width // DT
    flat = lambda *shape: jax.ShapeDtypeStruct(shape, BF16)
    any_ = pl.BlockSpec(memory_space=pl.ANY)
    dma = pltpu.SemaphoreType.DMA
    return pl.pallas_call(
        functools.partial(backward_reduce_scatter, n, axis),
        out_shape=(flat(rows, hidden), flat(rows, hidden), flat(rows, hidden), flat(half, width), flat(half, width)),
        in_specs=[any_] * 6,
        out_specs=(any_,) * 5,
        scratch_shapes=[
            pltpu.VMEM((2, 2 * UNIT, width), BF16),
            pltpu.VMEM((2, 2 * UNIT, hidden), BF16),
            pltpu.VMEM((2, 2 * UNIT, hidden), BF16),
            pltpu.VMEM((2 * UNIT, hidden), BF16),
            pltpu.VMEM((2 * UNIT, hidden), BF16),
            pltpu.VMEM((2 * UNIT, hidden), BF16),
            pltpu.VMEM((width, hidden), BF16),
            pltpu.VMEM((width, hidden), BF16),
            pltpu.VMEM((hidden, width), BF16),
            pltpu.VMEM((2, n, units, pieces, UNIT, DT), BF16),
            dma((2, 2, 3)), dma((2, 3)), dma((groups, 2)), dma((2, units, pieces)),
            dma((2, n - 1, units, pieces)), dma((2, n - 1, units, pieces)),
        ],
        compiler_params=pltpu.CompilerParams(
            collective_id=0, has_side_effects=True, vmem_limit_bytes=VMEM_LIMIT),
        cost_estimate=pl.CostEstimate(
            flops=6 * rows * width * hidden, transcendentals=rows * hidden,
            bytes_accessed=2 * (rows * width + 5 * rows * hidden + 3 * width * hidden)),
        name="dx_reduce_scatter",
    )(dy, gate, up, wg, wu, wd)


def copies(n, axis, shifts, srcs, out_ref, buf, in_sem, out_sem):
    half = buf.shape[1]
    me = lax.axis_index(axis)
    ins, outs = [], []
    for k, (shift, low) in enumerate(shifts):
        start = pl.multiple_of((2 * lax.rem(me + shift, n) + low) * half, half)
        ins.append(pltpu.make_async_copy(srcs[k], buf.at[k], in_sem.at[k]))
        outs.append(pltpu.make_async_copy(buf.at[k], out_ref.at[pl.ds(start, half)], out_sem.at[k]))
    return ins, outs


def dw_body(n, axis, shifts, a_ref, b_ref, *refs):
    count = len(shifts)
    srcs = refs[:count]
    o_ref, dx_ref, b_v, buf, b_sem, in_sem, out_sem = refs[-7:]
    cols = b_ref.shape[1]
    parts = cols // CT
    i, last = pl.program_id(0), pl.num_programs(0) - 1
    ins, outs = copies(n, axis, shifts, srcs, dx_ref, buf, in_sem, out_sem)
    loads = [pltpu.make_async_copy(b_ref.at[:, pl.ds(j * CT, CT)], b_v.at[:, pl.ds(j * CT, CT)], b_sem.at[j])
             for j in range(parts)]

    @pl.when(i == 0)
    def _():
        loads[0].start()
        loads[1].start()

    @pl.when(i == 1)
    def _():
        for copy in ins:
            copy.start()

    @pl.when(i == 2)
    def _():
        for copy in ins:
            copy.wait()
        for copy in outs:
            copy.start()

    def column(j):
        at = pl.ds(j * CT, CT)
        o_ref[:, at] = dot_tn(a_ref[...], b_v[:, at]).astype(BF16)

    @pl.when(i == 0)
    def _():
        for j in range(parts):
            loads[j].wait()
            if j + 2 < parts:
                loads[j + 2].start()
            column(j)

    @pl.when(i > 0)
    def _():
        for j in range(parts):
            column(j)

    @pl.when(i == last)
    def _():
        for copy in outs:
            copy.wait()


def dw_call(n, axis, a, b, shifts, pieces, dx):
    rows, m = a.shape
    cols = b.shape[1]
    half, width = pieces[0].shape
    count = len(pieces)
    any_ = pl.BlockSpec(memory_space=pl.ANY)
    extra = () if dx is None else (dx,)
    dma = pltpu.SemaphoreType.DMA
    return pl.pallas_call(
        functools.partial(dw_body, n, axis, shifts),
        grid=(m // MT,),
        out_shape=(jax.ShapeDtypeStruct((m, cols), BF16), jax.ShapeDtypeStruct((rows, width), BF16)),
        in_specs=[pl.BlockSpec((rows, MT), lambda i: (0, i)), any_] + [any_] * (count + len(extra)),
        out_specs=(pl.BlockSpec((MT, cols), lambda i: (i, 0)), any_),
        scratch_shapes=[pltpu.VMEM((rows, cols), BF16), pltpu.VMEM((count, half, width), BF16),
                        dma((cols // CT,)), dma((count,)), dma((count,))],
        input_output_aliases={2 + count: 1} if extra else {},
        compiler_params=pltpu.CompilerParams(vmem_limit_bytes=VMEM_LIMIT),
        cost_estimate=pl.CostEstimate(
            flops=2 * rows * m * cols, transcendentals=0,
            bytes_accessed=2 * (rows * m + rows * cols + m * cols)),
    )(a, b, *pieces, *extra)


def place_body(n, axis, shifts, *refs):
    count = len(shifts)
    out_ref, buf, in_sem, out_sem = refs[count + 1:]
    ins, outs = copies(n, axis, shifts, refs[:count], out_ref, buf, in_sem, out_sem)
    for copy in ins:
        copy.start()
    for i, o in zip(ins, outs):
        i.wait()
        o.start()
    for copy in outs:
        copy.wait()


def place_call(n, axis, shifts, pieces, dx):
    any_ = pl.BlockSpec(memory_space=pl.ANY)
    half, width = pieces[0].shape
    count = len(pieces)
    dma = pltpu.SemaphoreType.DMA
    return pl.pallas_call(
        functools.partial(place_body, n, axis, shifts),
        out_shape=jax.ShapeDtypeStruct(dx.shape, BF16),
        in_specs=[any_] * (count + 1),
        out_specs=any_,
        scratch_shapes=[pltpu.VMEM((count, half, width), BF16), dma((count,)), dma((count,))],
        input_output_aliases={count: 0},
        compiler_params=pltpu.CompilerParams(vmem_limit_bytes=VMEM_LIMIT),
        cost_estimate=pl.CostEstimate(flops=200 * count * half * width, transcendentals=0, bytes_accessed=4 * count * half * width),
    )(*pieces, dx)


def solution(mesh):
    axis = "tp"
    n = mesh.shape[axis]
    to_right = [(i, (i + 1) % n) for i in range(n)]
    to_left = [(i, (i + n - 1) % n) for i in range(n)]

    def send(part, pairs):
        return lax.ppermute(part, axis, pairs)

    def step(x, dy, gate, up, w_gate, w_up, w_down):
        d_gate, d_up, hid, top, bot = reduce_scatter_call(n, axis, dy, gate, up, w_gate, w_up, w_down)
        left_top = send(top, to_right)
        right_bot = send(bot, to_left)
        left_bot = send(bot, to_right)
        right_top = send(top, to_left)
        dw_gate, dx = dw_call(n, axis, x, d_gate, ((0, 0), (0, 1)), (top, bot), None)
        far_top = send(left_top, to_right)
        far_bot = send(right_bot, to_left)
        dw_up, dx = dw_call(n, axis, x, d_up, ((n - 1, 0), (1, 1)), (left_top, right_bot), dx)
        dw_down, dx = dw_call(n, axis, hid, dy, ((n - 1, 1), (1, 0)), (left_bot, right_top), dx)
        dx = place_call(n, axis, ((2, 0), (2, 1)), (far_top, far_bot), dx)
        return dx, dw_gate, dw_up, dw_down

    tokens, columns, rows = P("dp", None), P(None, "tp"), P("tp", None)
    return jax.shard_map(
        step,
        mesh=mesh,
        in_specs=(tokens, tokens, P("dp", "tp"), P("dp", "tp"), columns, columns, rows),
        out_specs=(tokens, P("dp", "tp"), P("dp", "tp"), P(("dp", "tp"), None)),
        check_vma=False,
    )
```

time: 369 us -> 261 us (0.71); the launches traced: 362 us -> 261 us
  matrix products: 221 us -> 0 us
  Pallas kernels: 0 us -> 221 us
  waiting for transfers between devices: 82.9 us -> 31.6 us
  local copies, waits for them, and re-layouts: 43.7 us -> 0 us
  between operations: 14.3 us -> 0.88 us
  starting transfers between devices: 0.06 us -> 7.37 us
    dot_general x6 -> x0, matrix products: 221 us -> none  [the longest x1 43.2 us: step(): d_hidden = jnp.dot(dy, w_down.T, preferred_element_type=jnp.float32)]
    pallas_call x0 -> x5, Pallas kernels: none -> 221 us  [the longest x1 119 us: reduce_scatter_call(): pl.pallas_call(functools.partial(backward_reduce_scatter, n, axis), out_s...]
    psum x1 -> x0, waiting for transfers between devices: 82.9 us -> none  [step(): dx = lax.psum(term.astype(jnp.bfloat16), 'tp')]
    unnamed x5 -> x0, local copies, waits for them, and re-layouts: 43.7 us -> none
    ppermute x0 -> x6, waiting for transfers between devices: none -> 31.6 us  [send(): return lax.ppermute(part, axis, pairs)]
    ppermute x0 -> x6, starting transfers between devices: none -> 7.37 us  [send(): return lax.ppermute(part, axis, pairs)]
  transfers between devices with their start and end apart: 1 -> 6, of which waited for: 1 -> 2; matrix products, arithmetic and copies ran while one was open for 39% -> 0% of each run, Pallas kernels for 0% -> 38%
where the time goes in v1:
time: 261 us
  Pallas kernels  221 us (85%)
  waiting for transfers between devices  31.6 us (12%)
  starting transfers between devices  7.37 us (3%)
    pallas_call x1, Pallas kernels, reduce_scatter_call(): pl.pallas_call(functools.partial(backward_reduce_scatter, n, axis), out_s...  119 us
    pallas_call x3, Pallas kernels, dw_call(): pl.pallas_call(functools.partial(dw_body, n, axis, shifts), grid=(m // MT...  98.5 us
    ppermute x6, waiting for transfers between devices, send(): return lax.ppermute(part, axis, pairs)  31.6 us
    ppermute x6, starting transfers between devices, send(): return lax.ppermute(part, axis, pairs)  7.37 us
  transfers between devices with their start and end apart: 6, of which 2 were waited for; matrix products, arithmetic and copies ran while one was open for 0% of the time, Pallas kernels for 38%

profile of v1, /device:TPU:112, one launch (start us, length us, event | category | flops | bytes accessed | tf_op | source)
XLA Modules:
  0.0 260.8 jit_solution(12909886052257367682)
XLA Ops:
  0.6 119.3 %dx_reduce_scatter.1 = (bf16[2048,2048]{1,0:T(8,128)(2,1)}, bf16[2048,2048]{1,0:T(8,128)(2,1)}, bf16[2048,2048]{1,0:T(8,128)(2,1)}, bf16[256,3072]{1,0:T(8,128)(2,1)}, bf16[256,3072]{1,0:T(8,128)(2,1)}) custom-call(bf16[2048,3072]{1,0:T(8,128)(2,1)} %b_ref.1, bf16[2048,2048]{1,0:T(8,128)(2,1)} %gate_ref.1, bf16[2048,2048]{1,0:T(8,128)(2,1)} %up_ref.1, ...), custom_call_target="tpu_custom_call" | custom-call | flops 77309411328 | bytes 92274688 | tf_op jit(solution)/shard_map/dx_reduce_scatter/pallas_call | solution.py:193
  119.9 0.8 collective-permute-start.5
  120.7 1.3 collective-permute-start
  122.0 0.1 collective-permute-start.4
  122.1 3.1 %collective-permute-start.2 = (bf16[256,3072]{1,0:T(8,128)(2,1)}, bf16[256,3072]{1,0:T(8,128)(2,1)}, u32[]{:S(2)}, u32[]{:S(2)}) collective-permute-start(bf16[256,3072]{1,0:T(8,128)(2,1)} %get-tuple-element.16.refs_1_), channel_id=1, source_target_pairs={{0,3},{1,0},{2,1},{3,2},{4,7},{5,4},{6,5},{7,6},{8,11},{9,8},{10,9... | collective-permute-start | bytes 4718600 | tf_op jit(solution)/shard_map/ppermute | solution.py:344
  125.3 32.7 %shard_map.102 = (bf16[3072,2048]{1,0:T(8,128)(2,1)}, bf16[2048,3072]{1,0:T(8,128)(2,1)}) custom-call(bf16[2048,3072]{1,0:T(8,128)(2,1)} %a_ref.3, bf16[2048,2048]{1,0:T(8,128)(2,1)} %get-tuple-element.19.b_ref, bf16[256,3072]{1,0:T(8,128)(2,1)} %get-tuple-element.15.refs_0_, bf16[256,3072]{1,0:T(8,128)(2,1)} %get-tuple-element.16.refs_1_), custom_call_target="tpu_custom_call" | custom-call | flops 25769803776 | bytes 33554432 | tf_op jit(solution)/shard_map/pallas_call | solution.py:291
  158.0 1.5 collective-permute-done.refs_0_
  159.5 0.1 collective-permute-start.1
  159.6 30.0 %collective-permute-done.2.refs_1_ = bf16[256,3072]{1,0:T(8,128)(2,1)} collective-permute-done((bf16[256,3072]{1,0:T(8,128)(2,1)}, bf16[256,3072]{1,0:T(8,128)(2,1)}, u32[]{:S(2)}, u32[]{:S(2)}) %collective-permute-start.2) | collective-permute-done | bytes 1572896 | tf_op jit(solution)/shard_map/ppermute | solution.py:344
  189.6 1.9 collective-permute-start.3
  191.6 32.7 %shard_map.103 = (bf16[3072,2048]{1,0:T(8,128)(2,1)}, bf16[2048,3072]{1,0:T(8,128)(2,1)}) custom-call(bf16[2048,3072]{1,0:T(8,128)(2,1)} %a_ref.3, bf16[2048,2048]{1,0:T(8,128)(2,1)} %get-tuple-element.18.b_ref, bf16[256,3072]{1,0:T(8,128)(2,1)} %collective-permute-done.refs_0_, ...), custom_call_target="tpu_custom_call", output_to_operand_aliasing={{1}: (4, {})} | custom-call | flops 25769803776 | bytes 33554432 | tf_op jit(solution)/shard_map/pallas_call | solution.py:291
  224.3 0.0 collective-permute-done.5.refs_1_
  224.3 0.0 collective-permute-done.4.refs_0_
  224.3 33.2 %shard_map.104 = (bf16[2048,3072]{1,0:T(8,128)(2,1)}, bf16[2048,3072]{1,0:T(8,128)(2,1)}) custom-call(bf16[2048,2048]{1,0:T(8,128)(2,1)} %get-tuple-element.17.a_ref, bf16[2048,3072]{1,0:T(8,128)(2,1)} %b_ref.1, bf16[256,3072]{1,0:T(8,128)(2,1)} %collective-permute-done.4.refs_0_, ...), custom_call_target="tpu_custom_call", output_to_operand_aliasing={{1}: (4, {})} | custom-call | flops 25769803776 | bytes 33554432 | tf_op jit(solution)/shard_map/pallas_call | solution.py:291
  257.5 0.0 collective-permute-done.1.refs_0_
  257.5 0.0 collective-permute-done.3.refs_1_
  257.5 3.1 %shard_map.105 = bf16[2048,3072]{1,0:T(8,128)(2,1)} custom-call(bf16[256,3072]{1,0:T(8,128)(2,1)} %collective-permute-done.1.refs_0_, bf16[256,3072]{1,0:T(8,128)(2,1)} %collective-permute-done.3.refs_1_, bf16[2048,3072]{1,0:T(8,128)(2,1)} %get-tuple-element.22.refs_2_), custom_call_target="tpu_custom_call", output_to_operand_aliasing={{}: (2, {})} | custom-call | flops 314572800 | bytes 6291456 | tf_op jit(solution)/shard_map/pallas_call | solution.py:325
Async XLA Ops:
  119.9 104.3 %collective-permute-start.5 = (bf16[256,3072]{1,0:T(8,128)(2,1)}, bf16[256,3072]{1,0:T(8,128)(2,1)}, u32[]{:S(2)}, u32[]{:S(2)}) collective-permute-start(bf16[256,3072]{1,0:T(8,128)(2,1)} %get-tuple-element.15.refs_0_), channel_id=1, source_target_pairs={{0,3},{1,0},{2,1},{3,2},{4,7},{5,4},{6,5},{7,6},{8,11},{9,8},{10,9... | collective-permute-start | bytes 4718600 | tf_op jit(solution)/shard_map/ppermute | solution.py:344
  120.7 38.8 %collective-permute-start = (bf16[256,3072]{1,0:T(8,128)(2,1)}, bf16[256,3072]{1,0:T(8,128)(2,1)}, u32[]{:S(2)}, u32[]{:S(2)}) collective-permute-start(bf16[256,3072]{1,0:T(8,128)(2,1)} %get-tuple-element.15.refs_0_), channel_id=1, source_target_pairs={{0,1},{1,2},{2,3},{3,0},{4,5},{5,6},{6,7},{7,4},{8,9},{9,10},{10,1... | collective-permute-start | bytes 4718600 | tf_op jit(solution)/shard_map/ppermute | solution.py:344
  122.0 102.2 %collective-permute-start.4 = (bf16[256,3072]{1,0:T(8,128)(2,1)}, bf16[256,3072]{1,0:T(8,128)(2,1)}, u32[]{:S(2)}, u32[]{:S(2)}) collective-permute-start(bf16[256,3072]{1,0:T(8,128)(2,1)} %get-tuple-element.16.refs_1_), channel_id=1, source_target_pairs={{0,1},{1,2},{2,3},{3,0},{4,5},{5,6},{6,7},{7,4},{8,9},{9,10},{10,1... | collective-permute-start | bytes 4718600 | tf_op jit(solution)/shard_map/ppermute | solution.py:344
  122.1 67.5 %collective-permute-start.2 = (bf16[256,3072]{1,0:T(8,128)(2,1)}, bf16[256,3072]{1,0:T(8,128)(2,1)}, u32[]{:S(2)}, u32[]{:S(2)}) collective-permute-start(bf16[256,3072]{1,0:T(8,128)(2,1)} %get-tuple-element.16.refs_1_), channel_id=1, source_target_pairs={{0,3},{1,0},{2,1},{3,2},{4,7},{5,4},{6,5},{7,6},{8,11},{9,8},{10,9... | collective-permute-start | bytes 4718600 | tf_op jit(solution)/shard_map/ppermute | solution.py:344
  159.5 98.0 %collective-permute-start.1 = (bf16[256,3072]{1,0:T(8,128)(2,1)}, bf16[256,3072]{1,0:T(8,128)(2,1)}, u32[]{:S(2)}, u32[]{:S(2)}) collective-permute-start(bf16[256,3072]{1,0:T(8,128)(2,1)} %collective-permute-done.refs_0_), channel_id=1, source_target_pairs={{0,1},{1,2},{2,3},{3,0},{4,5},{5,6},{6,7},{7,4},{8,9},{9,10},{10,1... | collective-permute-start | bytes 4718600 | tf_op jit(solution)/shard_map/ppermute | solution.py:344
  189.6 67.8 %collective-permute-start.3 = (bf16[256,3072]{1,0:T(8,128)(2,1)}, bf16[256,3072]{1,0:T(8,128)(2,1)}, u32[]{:S(2)}, u32[]{:S(2)}) collective-permute-start(bf16[256,3072]{1,0:T(8,128)(2,1)} %collective-permute-done.2.refs_1_), channel_id=1, source_target_pairs={{0,3},{1,0},{2,1},{3,2},{4,7},{5,4},{6,5},{7,6},{8,11},{9,8},{10,9... | collective-permute-start | bytes 4718600 | tf_op jit(solution)/shard_map/ppermute | solution.py:344
